TPU v7x, 32 devices: a whole 2x2x4 slice. The times are simulated.
32 devices in a mesh: groups: 2 (over x), seq: 16 (over z, y, core).
Axes of the slice: x: 2, y: 2, z: 4, core: 2. Of those that a mesh axis runs over, the one named last changes fastest.
Arguments:
- queries: bfloat16 [1024, 2048], P(('groups', 'seq')), parts along dimension 0, may hold values from -132 to 132
- fresh_keys: bfloat16 [1024, 2048], P(('groups', 'seq')), parts along dimension 0, may hold values from -6 to 6
- fresh_values: bfloat16 [1024, 2048], P(('groups', 'seq')), parts along dimension 0, may hold values from -48 to 48
- stale_keys: bfloat16 [1024, 2048], P(('groups', 'seq')), parts along dimension 0, may hold values from -6 to 6
- stale_values: bfloat16 [1024, 2048], P(('groups', 'seq')), parts along dimension 0, may hold values from -48 to 48
- patch_sizes: int32 [8], P('groups'), parts along dimension 0, may hold values from 1 to 256, 512 in all
Outputs:
- attended: bfloat16 [1024, 2048], P(('groups', 'seq')), parts along dimension 0
There are 2 independent parts, one for each index of `groups`. A program takes and returns all parts, laid end to end along the dimension named above; each array names one. Nothing has to cross between parts.
Inputs may be any that keep to these rules, and one draw needn't show every extreme that they name: `patch_sizes`: the patch lengths sum to 512.
All inputs are finite; a program needn't handle non-finite values.
Results may differ from a plain program's by a relative error of at most 0.006.
Values may be sent and summed in bfloat16 or wider, within the bound.
A program may use at most 64 MiB of HBM per device.

v0:
```python
import jax
import jax.numpy as jnp
from jax import lax
from jax.sharding import PartitionSpec as P

H = 16


def shifted(block, axis, distance):
    devices = range(lax.axis_size(axis))
    route = [((i - distance) % len(devices), i) for i in devices]
    return lax.ppermute(block, axis, route)


def shards(queries, fresh_keys, fresh_values, stale_keys, stale_values, patch_sizes):
    local_rows, columns = queries.shape
    head_size = columns // H
    devices = lax.axis_size("seq")
    query_groups = devices // H
    sub_rows = local_rows // query_groups
    shape_in = (sub_rows, devices, head_size)
    moved = (
        lax.all_to_all(queries.reshape(shape_in), "seq", split_axis=1, concat_axis=0, tiled=True),
        lax.all_to_all(
            fresh_keys.reshape(shape_in), "seq", split_axis=1, concat_axis=0, tiled=True
        ),
        lax.all_to_all(
            fresh_values.reshape(shape_in), "seq", split_axis=1, concat_axis=0, tiled=True
        ),
        lax.all_to_all(
            stale_keys.reshape(shape_in), "seq", split_axis=1, concat_axis=0, tiled=True
        ),
        lax.all_to_all(
            stale_values.reshape(shape_in), "seq", split_axis=1, concat_axis=0, tiled=True
        ),
    )
    query_rows = moved[0].reshape(-1, head_size)
    stacked = jnp.stack(
        [
            moved[1].reshape(-1, head_size),
            moved[2].reshape(-1, head_size),
            moved[3].reshape(-1, head_size),
            moved[4].reshape(-1, head_size),
        ]
    )
    own_group = lax.axis_index("seq") // H
    patch_ends = jnp.cumsum(patch_sizes)[:-1]
    positions = (
        jnp.arange(devices, dtype=jnp.int32)[:, None] * local_rows
        + jnp.arange(sub_rows, dtype=jnp.int32)[None, :] * query_groups
    ).reshape(-1)

    def patch_of(group):
        hits = positions[:, None] + group >= patch_ends[None, :]
        return jnp.sum(hits.astype(jnp.int32), axis=1)

    score_scale = head_size ** (-0.5)
    contract = (((1,), (1,)), ((), ()))
    query_patch = patch_of(own_group)

    def absorb(carry_state, key_block, source_group):
        running_max, denominator, numerator = carry_state
        is_fresh = patch_of(source_group)[None, :] <= query_patch[:, None]
        fresh_scores = lax.dot_general(
            query_rows, key_block[0], contract, preferred_element_type=jnp.float32
        )
        stale_scores = lax.dot_general(
            query_rows, key_block[2], contract, preferred_element_type=jnp.float32
        )
        scores = jnp.where(is_fresh, fresh_scores, stale_scores) * score_scale
        new_max = jnp.maximum(running_max, jnp.max(scores, axis=1, keepdims=True))
        rescale = jnp.exp(running_max - new_max)
        weights = jnp.exp(scores - new_max)
        denominator = denominator * rescale + jnp.sum(weights, axis=1, keepdims=True)
        rounded = weights.astype(jnp.bfloat16)
        zeroes = jnp.zeros_like(rounded)
        numerator = numerator * rescale + jnp.dot(
            jnp.where(is_fresh, rounded, zeroes), key_block[1], preferred_element_type=jnp.float32
        )
        numerator = numerator + jnp.dot(
            jnp.where(is_fresh, zeroes, rounded), key_block[3], preferred_element_type=jnp.float32
        )
        return (new_max, denominator, numerator)

    query_count = query_rows.shape[0]
    carry_state = (
        jnp.full((query_count, 1), -1e30, jnp.float32),
        jnp.zeros((query_count, 1), jnp.float32),
        jnp.zeros((query_count, head_size), jnp.float32),
    )
    carry_state = absorb(carry_state, stacked, own_group)
    travelling = stacked
    for offset in range(1, query_groups):
        travelling = shifted(travelling, "seq", H)
        carry_state = absorb(carry_state, travelling, (own_group - offset) % query_groups)
    attended = (carry_state[2] / carry_state[1]).astype(jnp.bfloat16)
    returned = lax.all_to_all(
        attended.reshape(devices, sub_rows, 1, head_size),
        "seq",
        split_axis=0,
        concat_axis=2,
        tiled=True,
    )
    return returned.reshape(local_rows, columns)


def solution(mesh):
    in_specs = (
        P(("groups", "seq"), None),
        P(("groups", "seq"), None),
        P(("groups", "seq"), None),
        P(("groups", "seq"), None),
        P(("groups", "seq"), None),
        P("groups"),
    )
    out_specs = P(("groups", "seq"), None)
    return jax.shard_map(shards, mesh=mesh, in_specs=in_specs, out_specs=out_specs, check_vma=False)
```

profile of v0, /device:TPU:0, one launch (start us, length us, event | category | flops | bytes accessed | tf_op | source)
XLA Modules:
  0.0 74.3 jit_solution(5553754712294257362)
XLA Ops:
  0.0 0.0 copy-start
  0.0 0.9 %copy-done = bf16[32,2048]{1,0:T(8,128)(2,1)S(1)} copy-done((bf16[32,2048]{1,0:T(8,128)(2,1)S(1)}, bf16[32,2048]{1,0:T(8,128)(2,1)}, u32[]{:S(2)}) %copy-start) | copy-done | bytes 131096
  0.9 0.7 copy_bitcast_fusion.5
  1.6 0.0 copy-start.1
  1.6 7.5 %all-to-all-start = ((bf16[32,16,128]{2,0,1:T(8,128)(2,1)}), bf16[32,16,128]{2,0,1:T(8,128)(2,1)S(1)}, u32[]{:S(2)}, u32[]{:S(2)}) async-start(bf16[32,16,128]{2,0,1:T(8,128)(2,1)} %copy_bitcast_fusion.5), calls=%async_computation | async-start | bytes 262144 | tf_op jit(solution)/shard_map/all_to_all | solution.py:23
  9.2 0.0 copy-start.5
  9.2 0.6 copy-done.5
  9.8 0.2 reduce-window.4
  10.0 0.0 copy-done.1
  10.0 0.0 copy-start.2
  10.0 0.7 copy_bitcast_fusion.4
  10.7 0.3 copy-done.2
  10.9 0.0 copy-start.3
  10.9 0.7 copy_bitcast_fusion.3
  11.6 0.1 add_add_fusion
  11.7 0.1 add.55
  11.8 0.1 copy-done.3
  11.9 0.7 copy_bitcast_fusion.2
  12.6 0.0 copy-start.4
  12.6 4.5 %all-to-all-done = bf16[32,16,128]{2,0,1:T(8,128)(2,1)S(1)} async-done(((bf16[32,16,128]{2,0,1:T(8,128)(2,1)}), bf16[32,16,128]{2,0,1:T(8,128)(2,1)S(1)}, u32[]{:S(2)}, u32[]{:S(2)}) %all-to-all-start) | async-done | bytes 131104 | tf_op jit(solution)/shard_map/all_to_all | solution.py:23
  17.0 3.5 %all-to-all-start.1 = ((bf16[32,16,128]{2,0,1:T(8,128)(2,1)}), bf16[32,16,128]{2,0,1:T(8,128)(2,1)S(1)}, u32[]{:S(2)}, u32[]{:S(2)}) async-start(bf16[32,16,128]{2,0,1:T(8,128)(2,1)} %copy_bitcast_fusion.4), calls=%async_computation.1 | async-start | bytes 262144 | tf_op jit(solution)/shard_map/all_to_all | solution.py:24
  20.6 0.1 convert_reduce_fusion
  20.6 0.0 copy-done.4
  20.6 0.7 copy_bitcast_fusion.1
  21.3 7.1 %all-to-all-done.1 = bf16[32,16,128]{2,0,1:T(8,128)(2,1)S(1)} async-done(((bf16[32,16,128]{2,0,1:T(8,128)(2,1)}), bf16[32,16,128]{2,0,1:T(8,128)(2,1)S(1)}, u32[]{:S(2)}, u32[]{:S(2)}) %all-to-all-start.1) | async-done | bytes 131104 | tf_op jit(solution)/shard_map/all_to_all | solution.py:24
  28.4 3.5 %all-to-all-start.2 = ((bf16[32,16,128]{2,0,1:T(8,128)(2,1)}), bf16[32,16,128]{2,0,1:T(8,128)(2,1)S(1)}, u32[]{:S(2)}, u32[]{:S(2)}) async-start(bf16[32,16,128]{2,0,1:T(8,128)(2,1)} %copy_bitcast_fusion.3), calls=%async_computation.2 | async-start | bytes 262144 | tf_op jit(solution)/shard_map/all_to_all | solution.py:30
  31.9 0.3 fusion.17
  32.2 7.6 %all-to-all-done.2 = bf16[32,16,128]{2,0,1:T(8,128)(2,1)S(1)} async-done(((bf16[32,16,128]{2,0,1:T(8,128)(2,1)}), bf16[32,16,128]{2,0,1:T(8,128)(2,1)S(1)}, u32[]{:S(2)}, u32[]{:S(2)}) %all-to-all-start.2) | async-done | bytes 131104 | tf_op jit(solution)/shard_map/all_to_all | solution.py:30
  39.8 3.5 %all-to-all-start.3 = ((bf16[32,16,128]{2,0,1:T(8,128)(2,1)}), bf16[32,16,128]{2,0,1:T(8,128)(2,1)S(1)}, u32[]{:S(2)}, u32[]{:S(2)}) async-start(bf16[32,16,128]{2,0,1:T(8,128)(2,1)} %copy_bitcast_fusion.2), calls=%async_computation.3 | async-start | bytes 262144 | tf_op jit(solution)/shard_map/all_to_all | solution.py:27
  43.3 0.3 fusion.16
  43.7 0.2 fusion.3
  43.9 7.3 %all-to-all-done.3 = bf16[32,16,128]{2,0,1:T(8,128)(2,1)S(1)} async-done(((bf16[32,16,128]{2,0,1:T(8,128)(2,1)}), bf16[32,16,128]{2,0,1:T(8,128)(2,1)S(1)}, u32[]{:S(2)}, u32[]{:S(2)}) %all-to-all-start.3) | async-done | bytes 131104 | tf_op jit(solution)/shard_map/all_to_all | solution.py:27
  51.2 3.5 %all-to-all-start.4 = ((bf16[32,16,128]{2,0,1:T(8,128)(2,1)}), bf16[32,16,128]{2,0,1:T(8,128)(2,1)S(1)}, u32[]{:S(2)}, u32[]{:S(2)}) async-start(bf16[32,16,128]{2,0,1:T(8,128)(2,1)} %copy_bitcast_fusion.1), calls=%async_computation.4 | async-start | bytes 262144 | tf_op jit(solution)/shard_map/all_to_all | solution.py:33
  54.7 0.4 convolution_add_fusion.1
  55.2 7.4 %all-to-all-done.4 = bf16[32,16,128]{2,0,1:T(8,128)(2,1)S(1)} async-done(((bf16[32,16,128]{2,0,1:T(8,128)(2,1)}), bf16[32,16,128]{2,0,1:T(8,128)(2,1)S(1)}, u32[]{:S(2)}, u32[]{:S(2)}) %all-to-all-start.4) | async-done | bytes 131104 | tf_op jit(solution)/shard_map/all_to_all | solution.py:33
  62.6 0.5 fusion.2
  63.1 10.5 %all_to_all.90 = bf16[16,32,1,128]{3,1,2,0:T(8,128)(2,1)S(1)} all-to-all(bf16[16,32,1,128]{3,1,2,0:T(8,128)(2,1)S(1)} %bitcast.79), channel_id=1, replica_groups=mesh['groups'=2,'seq'=16] {'seq'}, dimensions={0} | all-to-all | bytes 262144 | tf_op jit(solution)/shard_map/all_to_all | solution.py:97
  73.6 0.1 copy.34
  73.6 0.7 copy.47
  (4 shorter events, 0.0 us)
Async XLA Ops:
  0.0 0.9 %copy-start = (bf16[32,2048]{1,0:T(8,128)(2,1)S(1)}, bf16[32,2048]{1,0:T(8,128)(2,1)}, u32[]{:S(2)}) copy-start(bf16[32,2048]{1,0:T(8,128)(2,1)} %param.6) | copy-start | bytes 393220
  1.6 8.4 %copy-start.1 = (bf16[32,2048]{1,0:T(8,128)(2,1)S(1)}, bf16[32,2048]{1,0:T(8,128)(2,1)}, u32[]{:S(2)}) copy-start(bf16[32,2048]{1,0:T(8,128)(2,1)} %param.7) | copy-start | bytes 393220
  1.6 15.5 %all-to-all-start = ((bf16[32,16,128]{2,0,1:T(8,128)(2,1)}), bf16[32,16,128]{2,0,1:T(8,128)(2,1)S(1)}, u32[]{:S(2)}, u32[]{:S(2)}) async-start(bf16[32,16,128]{2,0,1:T(8,128)(2,1)} %copy_bitcast_fusion.5), calls=%async_computation | async-start | bytes 262144 | tf_op jit(solution)/shard_map/all_to_all | solution.py:23
  9.2 0.7 copy-start.5
  10.0 1.0 %copy-start.2 = (bf16[32,2048]{1,0:T(8,128)(2,1)S(1)}, bf16[32,2048]{1,0:T(8,128)(2,1)}, u32[]{:S(2)}) copy-start(bf16[32,2048]{1,0:T(8,128)(2,1)} %param.9) | copy-start | bytes 393220
  10.9 1.0 %copy-start.3 = (bf16[32,2048]{1,0:T(8,128)(2,1)S(1)}, bf16[32,2048]{1,0:T(8,128)(2,1)}, u32[]{:S(2)}) copy-start(bf16[32,2048]{1,0:T(8,128)(2,1)} %param.8) | copy-start | bytes 393220
  12.6 8.1 %copy-start.4 = (bf16[32,2048]{1,0:T(8,128)(2,1)S(1)}, bf16[32,2048]{1,0:T(8,128)(2,1)}, u32[]{:S(2)}) copy-start(bf16[32,2048]{1,0:T(8,128)(2,1)} %param.10) | copy-start | bytes 393220
  17.0 11.4 %all-to-all-start.1 = ((bf16[32,16,128]{2,0,1:T(8,128)(2,1)}), bf16[32,16,128]{2,0,1:T(8,128)(2,1)S(1)}, u32[]{:S(2)}, u32[]{:S(2)}) async-start(bf16[32,16,128]{2,0,1:T(8,128)(2,1)} %copy_bitcast_fusion.4), calls=%async_computation.1 | async-start | bytes 262144 | tf_op jit(solution)/shard_map/all_to_all | solution.py:24
  28.4 11.4 %all-to-all-start.2 = ((bf16[32,16,128]{2,0,1:T(8,128)(2,1)}), bf16[32,16,128]{2,0,1:T(8,128)(2,1)S(1)}, u32[]{:S(2)}, u32[]{:S(2)}) async-start(bf16[32,16,128]{2,0,1:T(8,128)(2,1)} %copy_bitcast_fusion.3), calls=%async_computation.2 | async-start | bytes 262144 | tf_op jit(solution)/shard_map/all_to_all | solution.py:30
  39.8 11.4 %all-to-all-start.3 = ((bf16[32,16,128]{2,0,1:T(8,128)(2,1)}), bf16[32,16,128]{2,0,1:T(8,128)(2,1)S(1)}, u32[]{:S(2)}, u32[]{:S(2)}) async-start(bf16[32,16,128]{2,0,1:T(8,128)(2,1)} %copy_bitcast_fusion.2), calls=%async_computation.3 | async-start | bytes 262144 | tf_op jit(solution)/shard_map/all_to_all | solution.py:27
  51.2 11.4 %all-to-all-start.4 = ((bf16[32,16,128]{2,0,1:T(8,128)(2,1)}), bf16[32,16,128]{2,0,1:T(8,128)(2,1)S(1)}, u32[]{:S(2)}, u32[]{:S(2)}) async-start(bf16[32,16,128]{2,0,1:T(8,128)(2,1)} %copy_bitcast_fusion.1), calls=%async_computation.4 | async-start | bytes 262144 | tf_op jit(solution)/shard_map/all_to_all | solution.py:33
where the time goes:
time: 74.9 us; the launch traced here: 74.3 us
  waiting for transfers between devices  33.9 us (45%)
  starting transfers between devices  21.6 us (29%)
  blocking collectives  10.5 us (14%)
  local copies, waits for them, and re-layouts  6.15 us (8%)
  matrix products  1.53 us (2%)
    all_to_all x1, blocking collectives, shards(): lax.all_to_all(attended.reshape(devices, sub_rows, 1, head_size), 'seq',...  10.5 us
    all_to_all x1, waiting for transfers between devices, shards(): lax.all_to_all(stale_keys.reshape(shape_in), 'seq', split_axis=1, concat_...  7.57 us
    all_to_all x1, starting transfers between devices, shards(): lax.all_to_all(queries.reshape(shape_in), 'seq', split_axis=1, concat_axi...  7.55 us
    all_to_all x1, waiting for transfers between devices, shards(): lax.all_to_all(stale_values.reshape(shape_in), 'seq', split_axis=1, conca...  7.43 us
    all_to_all x1, waiting for transfers between devices, shards(): lax.all_to_all(fresh_values.reshape(shape_in), 'seq', split_axis=1, conca...  7.33 us
    all_to_all x1, waiting for transfers between devices, shards(): lax.all_to_all(fresh_keys.reshape(shape_in), 'seq', split_axis=1, concat_...  7.11 us
    all_to_all x1, waiting for transfers between devices, shards(): lax.all_to_all(queries.reshape(shape_in), 'seq', split_axis=1, concat_axi...  4.46 us
    all_to_all x1, starting transfers between devices, shards(): lax.all_to_all(fresh_values.reshape(shape_in), 'seq', split_axis=1, conca...  3.51 us
  transfers between devices with their start and end apart: 5, of which 5 were waited for; matrix products, arithmetic and copies ran while one was open for 6% of the time, Pallas kernels for 0%

commit v1 on v0

--- a/solution.py
+++ b/solution.py
@@ -1,9 +1,25 @@
+import functools
 import jax
 import jax.numpy as jnp
 from jax import lax
 from jax.sharding import PartitionSpec as P
 
 H = 16
+
+
+def form_frame_up(u, comm_axis):
+    return jnp.concatenate(
+        lax.all_to_all(
+            jnp.stack(jnp.split(u, lax.axis_size(comm_axis), 1), 0),
+            axis_name=comm_axis,
+            concat_axis=0,
+            split_axis=0,
+        ),
+        0,
+    )
+
+
+build_teams_over_axis = functools.partial(form_frame_up, comm_axis="seq")
 
 
 def shifted(block, axis, distance):
@@ -24,9 +40,7 @@
         lax.all_to_all(
             fresh_keys.reshape(shape_in), "seq", split_axis=1, concat_axis=0, tiled=True
         ),
-        lax.all_to_all(
-            fresh_values.reshape(shape_in), "seq", split_axis=1, concat_axis=0, tiled=True
-        ),
+        build_teams_over_axis(fresh_values.reshape(shape_in)),
         lax.all_to_all(
             stale_keys.reshape(shape_in), "seq", split_axis=1, concat_axis=0, tiled=True
         ),

time: 74.9 us -> 82.2 us (1.097)
  local copies, waits for them, and re-layouts: 6.15 us -> 15.3 us
  waiting for transfers between devices: 33.9 us -> 29.5 us
  starting transfers between devices: 21.6 us -> 24.2 us
    unnamed x13 -> x29, local copies, waits for them, and re-layouts: 2.66 us -> 11.6 us
    all_to_all x1, waiting for transfers between devices: 4.46 us -> 0.01 us  [shards(): lax.all_to_all(queries.reshape(shape_in), 'seq', split_axis=1, concat_axi...]
    all_to_all x1, starting transfers between devices: 3.51 us -> 6.13 us  [shards(): lax.all_to_all(fresh_keys.reshape(shape_in), 'seq', split_axis=1, concat_...]
  transfers between devices with their start and end apart: 5 -> 5, of which waited for: 5 -> 4; matrix products, arithmetic and copies ran while one was open for 6% -> 17% of each run, Pallas kernels for 0% -> 0%
where the time goes in v1:
time: 82.2 us; the launch traced here: 81.7 us
  waiting for transfers between devices  29.5 us (36%)
  starting transfers between devices  24.2 us (29%)
  local copies, waits for them, and re-layouts  15.3 us (19%)
  blocking collectives  10.5 us (13%)
  matrix products  1.52 us (2%)
    unnamed x29, local copies, waits for them, and re-layouts  11.6 us
    all_to_all x1, blocking collectives, shards(): lax.all_to_all(attended.reshape(devices, sub_rows, 1, head_size), 'seq',...  10.5 us
    all_to_all x1, waiting for transfers between devices, shards(): lax.all_to_all(stale_keys.reshape(shape_in), 'seq', split_axis=1, concat_...  7.58 us
    all_to_all x1, starting transfers between devices, shards(): lax.all_to_all(queries.reshape(shape_in), 'seq', split_axis=1, concat_axi...  7.55 us
    all_to_all x1, waiting for transfers between devices, shards(): lax.all_to_all(stale_values.reshape(shape_in), 'seq', split_axis=1, conca...  7.43 us
    all_to_all x1, waiting for transfers between devices, form_frame_up(): lax.all_to_all(jnp.stack(jnp.split(u, lax.axis_size(comm_axis), 1), 0), a...  7.33 us
    all_to_all x1, waiting for transfers between devices, shards(): lax.all_to_all(fresh_keys.reshape(shape_in), 'seq', split_axis=1, concat_...  7.14 us
    all_to_all x1, starting transfers between devices, shards(): lax.all_to_all(fresh_keys.reshape(shape_in), 'seq', split_axis=1, concat_...  6.13 us
  transfers between devices with their start and end apart: 5, of which 4 were waited for; matrix products, arithmetic and copies ran while one was open for 17% of the time, Pallas kernels for 0%

profile of v1, /device:TPU:0, one launch (start us, length us, event | category | flops | bytes accessed | tf_op | source)
XLA Modules:
  0.0 81.7 jit_solution(17580012997980046588)
XLA Ops:
  0.0 0.0 copy-start
  0.0 0.9 %copy-done = bf16[32,2048]{1,0:T(8,128)(2,1)S(1)} copy-done((bf16[32,2048]{1,0:T(8,128)(2,1)S(1)}, bf16[32,2048]{1,0:T(8,128)(2,1)}, u32[]{:S(2)}) %copy-start) | copy-done | bytes 131096
  0.9 0.7 copy_bitcast_fusion.4
  1.6 0.0 copy-start.1
  1.6 7.5 %all-to-all-start = ((bf16[32,16,128]{2,0,1:T(8,128)(2,1)}), bf16[32,16,128]{2,0,1:T(8,128)(2,1)S(1)}, u32[]{:S(2)}, u32[]{:S(2)}) async-start(bf16[32,16,128]{2,0,1:T(8,128)(2,1)} %copy_bitcast_fusion.4), calls=%async_computation | async-start | bytes 262144 | tf_op jit(solution)/shard_map/all_to_all | solution.py:39
  9.2 0.0 copy-start.5
  9.2 0.6 copy-done.5
  9.8 0.2 reduce-window.4
  10.0 0.0 copy-done.1
  10.0 0.0 copy-start.2
  10.0 0.7 copy_bitcast_fusion.3
  10.7 0.3 copy-done.2
  11.0 0.3 fusion.16
  11.2 0.6 constant_dynamic-update-slice_fusion.15
  11.9 0.1 add_add_fusion
  11.9 0.6 constant_dynamic-update-slice_fusion.14
  12.5 0.6 constant_dynamic-update-slice_fusion.13
  13.1 0.6 constant_dynamic-update-slice_fusion.12
  13.7 0.6 constant_dynamic-update-slice_fusion.11
  14.3 0.6 constant_dynamic-update-slice_fusion.10
  14.9 0.6 constant_dynamic-update-slice_fusion.9
  15.5 0.0 copy-start.3
  15.5 0.6 constant_dynamic-update-slice_fusion.8
  16.1 0.6 constant_dynamic-update-slice_fusion.7
  16.7 0.6 constant_dynamic-update-slice_fusion.6
  17.3 0.6 constant_dynamic-update-slice_fusion.5
  17.9 0.6 constant_dynamic-update-slice_fusion.4
  18.5 0.6 constant_dynamic-update-slice_fusion.3
  19.1 0.6 constant_dynamic-update-slice_fusion.2
  19.7 0.6 constant_dynamic-update-slice_fusion.1
  20.3 0.6 constant_dynamic-update-slice_fusion
  20.9 0.1 add.55
  21.0 0.0 copy-done.3
  21.0 0.7 copy_bitcast_fusion.2
  21.7 0.0 copy-start.4
  21.7 0.0 all-to-all-done
  21.7 6.1 %all-to-all-start.1 = ((bf16[32,16,128]{2,0,1:T(8,128)(2,1)}), bf16[32,16,128]{2,0,1:T(8,128)(2,1)S(1)}, u32[]{:S(2)}, u32[]{:S(2)}) async-start(bf16[32,16,128]{2,0,1:T(8,128)(2,1)} %copy_bitcast_fusion.3), calls=%async_computation.1 | async-start | bytes 262144 | tf_op jit(solution)/shard_map/all_to_all | solution.py:40
  27.9 0.1 convert_reduce_fusion
  27.9 0.0 copy-done.4
  27.9 0.7 copy_bitcast_fusion.1
  28.6 7.1 %all-to-all-done.1 = bf16[32,16,128]{2,0,1:T(8,128)(2,1)S(1)} async-done(((bf16[32,16,128]{2,0,1:T(8,128)(2,1)}), bf16[32,16,128]{2,0,1:T(8,128)(2,1)S(1)}, u32[]{:S(2)}, u32[]{:S(2)}) %all-to-all-start.1) | async-done | bytes 131104 | tf_op jit(solution)/shard_map/all_to_all | solution.py:40
  35.8 3.5 %all-to-all-start.2 = ((bf16[32,16,128]{2,0,1:T(8,128)(2,1)}), bf16[32,16,128]{2,0,1:T(8,128)(2,1)S(1)}, u32[]{:S(2)}, u32[]{:S(2)}) async-start(bf16[32,16,128]{2,0,1:T(8,128)(2,1)} %copy_bitcast_fusion.2), calls=%async_computation.2 | async-start | bytes 262144 | tf_op jit(solution)/shard_map/all_to_all | solution.py:44
  39.3 0.3 fusion.18
  39.6 7.6 %all-to-all-done.2 = bf16[32,16,128]{2,0,1:T(8,128)(2,1)S(1)} async-done(((bf16[32,16,128]{2,0,1:T(8,128)(2,1)}), bf16[32,16,128]{2,0,1:T(8,128)(2,1)S(1)}, u32[]{:S(2)}, u32[]{:S(2)}) %all-to-all-start.2) | async-done | bytes 131104 | tf_op jit(solution)/shard_map/all_to_all | solution.py:44
  47.1 3.5 %all-to-all-start.3 = ((bf16[16,32,1,128]{3,1,2,0:T(8,128)(2,1)}), bf16[16,32,1,128]{3,1,2,0:T(8,128)(2,1)S(1)}, u32[]{:S(2)}, u32[]{:S(2)}) async-start(bf16[16,32,1,128]{3,1,2,0:T(8,128)(2,1)} %constant_dynamic-update-slice_fusion), calls=%async_computation.3 | async-start | bytes 262144 | tf_op jit(solution)/shard_map/all_to_all | solution.py:12
  50.7 0.3 fusion.17
  51.0 0.2 fusion.3
  51.2 7.3 %all-to-all-done.3 = bf16[16,32,1,128]{3,1,2,0:T(8,128)(2,1)S(1)} async-done(((bf16[16,32,1,128]{3,1,2,0:T(8,128)(2,1)}), bf16[16,32,1,128]{3,1,2,0:T(8,128)(2,1)S(1)}, u32[]{:S(2)}, u32[]{:S(2)}) %all-to-all-start.3) | async-done | bytes 131104 | tf_op jit(solution)/shard_map/all_to_all | solution.py:12
  58.5 3.5 %all-to-all-start.4 = ((bf16[32,16,128]{2,0,1:T(8,128)(2,1)}), bf16[32,16,128]{2,0,1:T(8,128)(2,1)S(1)}, u32[]{:S(2)}, u32[]{:S(2)}) async-start(bf16[32,16,128]{2,0,1:T(8,128)(2,1)} %copy_bitcast_fusion.1), calls=%async_computation.4 | async-start | bytes 262144 | tf_op jit(solution)/shard_map/all_to_all | solution.py:47
  62.1 0.4 convolution_add_fusion.1
  62.5 7.4 %all-to-all-done.4 = bf16[32,16,128]{2,0,1:T(8,128)(2,1)S(1)} async-done(((bf16[32,16,128]{2,0,1:T(8,128)(2,1)}), bf16[32,16,128]{2,0,1:T(8,128)(2,1)S(1)}, u32[]{:S(2)}, u32[]{:S(2)}) %all-to-all-start.4) | async-done | bytes 131104 | tf_op jit(solution)/shard_map/all_to_all | solution.py:47
  69.9 0.5 fusion.2
  70.4 10.5 %all_to_all.80 = bf16[16,32,1,128]{3,1,2,0:T(8,128)(2,1)S(1)} all-to-all(bf16[16,32,1,128]{3,1,2,0:T(8,128)(2,1)S(1)} %bitcast.106), channel_id=1, replica_groups=mesh['groups'=2,'seq'=16] {'seq'}, dimensions={0} | all-to-all | bytes 262144 | tf_op jit(solution)/shard_map/all_to_all | solution.py:111
  80.9 0.1 copy.225
  81.0 0.7 copy.269
  (5 shorter events, 0.0 us)
Async XLA Ops:
  0.0 0.9 %copy-start = (bf16[32,2048]{1,0:T(8,128)(2,1)S(1)}, bf16[32,2048]{1,0:T(8,128)(2,1)}, u32[]{:S(2)}) copy-start(bf16[32,2048]{1,0:T(8,128)(2,1)} %param.6) | copy-start | bytes 393220
  1.6 8.4 %copy-start.1 = (bf16[32,2048]{1,0:T(8,128)(2,1)S(1)}, bf16[32,2048]{1,0:T(8,128)(2,1)}, u32[]{:S(2)}) copy-start(bf16[32,2048]{1,0:T(8,128)(2,1)} %param.7) | copy-start | bytes 393220
  1.6 20.1 %all-to-all-start = ((bf16[32,16,128]{2,0,1:T(8,128)(2,1)}), bf16[32,16,128]{2,0,1:T(8,128)(2,1)S(1)}, u32[]{:S(2)}, u32[]{:S(2)}) async-start(bf16[32,16,128]{2,0,1:T(8,128)(2,1)} %copy_bitcast_fusion.4), calls=%async_computation | async-start | bytes 262144 | tf_op jit(solution)/shard_map/all_to_all | solution.py:39
  9.2 0.7 copy-start.5
  10.0 1.0 %copy-start.2 = (bf16[32,2048]{1,0:T(8,128)(2,1)S(1)}, bf16[32,2048]{1,0:T(8,128)(2,1)}, u32[]{:S(2)}) copy-start(bf16[32,2048]{1,0:T(8,128)(2,1)} %param.8) | copy-start | bytes 393220
  15.5 5.5 %copy-start.3 = (bf16[32,2048]{1,0:T(8,128)(2,1)S(1)}, bf16[32,2048]{1,0:T(8,128)(2,1)}, u32[]{:S(2)}) copy-start(bf16[32,2048]{1,0:T(8,128)(2,1)} %param.9) | copy-start | bytes 393220
  21.7 6.2 %copy-start.4 = (bf16[32,2048]{1,0:T(8,128)(2,1)S(1)}, bf16[32,2048]{1,0:T(8,128)(2,1)}, u32[]{:S(2)}) copy-start(bf16[32,2048]{1,0:T(8,128)(2,1)} %param.10) | copy-start | bytes 393220
  21.7 14.0 %all-to-all-start.1 = ((bf16[32,16,128]{2,0,1:T(8,128)(2,1)}), bf16[32,16,128]{2,0,1:T(8,128)(2,1)S(1)}, u32[]{:S(2)}, u32[]{:S(2)}) async-start(bf16[32,16,128]{2,0,1:T(8,128)(2,1)} %copy_bitcast_fusion.3), calls=%async_computation.1 | async-start | bytes 262144 | tf_op jit(solution)/shard_map/all_to_all | solution.py:40
  35.8 11.4 %all-to-all-start.2 = ((bf16[32,16,128]{2,0,1:T(8,128)(2,1)}), bf16[32,16,128]{2,0,1:T(8,128)(2,1)S(1)}, u32[]{:S(2)}, u32[]{:S(2)}) async-start(bf16[32,16,128]{2,0,1:T(8,128)(2,1)} %copy_bitcast_fusion.2), calls=%async_computation.2 | async-start | bytes 262144 | tf_op jit(solution)/shard_map/all_to_all | solution.py:44
  47.1 11.4 %all-to-all-start.3 = ((bf16[16,32,1,128]{3,1,2,0:T(8,128)(2,1)}), bf16[16,32,1,128]{3,1,2,0:T(8,128)(2,1)S(1)}, u32[]{:S(2)}, u32[]{:S(2)}) async-start(bf16[16,32,1,128]{3,1,2,0:T(8,128)(2,1)} %constant_dynamic-update-slice_fusion), calls=%async_computation.3 | async-start | bytes 262144 | tf_op jit(solution)/shard_map/all_to_all | solution.py:12
  58.5 11.4 %all-to-all-start.4 = ((bf16[32,16,128]{2,0,1:T(8,128)(2,1)}), bf16[32,16,128]{2,0,1:T(8,128)(2,1)S(1)}, u32[]{:S(2)}, u32[]{:S(2)}) async-start(bf16[32,16,128]{2,0,1:T(8,128)(2,1)} %copy_bitcast_fusion.1), calls=%async_computation.4 | async-start | bytes 262144 | tf_op jit(solution)/shard_map/all_to_all | solution.py:47
